TPU v7x, 256 devices: a 2x2x32 block of a 4x8x32 slice. The times are simulated.
256 devices in a mesh: groups: 4 (over y, x), tp: 32 (over z), sp: 2 (over core).
Axes of the slice: x: 2, y: 2, z: 32, core: 2. Of those that a mesh axis runs over, the one named last changes fastest.
The devices are a block of a 4x8x32 slice.
Arguments:
- tokens: bfloat16 [12288, 4608], P(('groups', 'tp', 'sp')), parts along dimension 0, may hold values from -48 to 48
- w_query: bfloat16 [4608, 4096], P(None, 'tp'), may hold values from -0.09375 to 0.09375
- w_key: bfloat16 [4608, 2048], P(None, 'tp'), may hold values from -0.09375 to 0.09375
- w_value: bfloat16 [4608, 2048], P(None, 'tp'), may hold values from -0.09375 to 0.09375
- w_out: bfloat16 [4096, 4608], P('tp'), may hold values from -0.5 to 0.5
- doc_lengths: int32 [32], P('groups'), parts along dimension 0, may hold values from 1 to 768, 3072 in all
Outputs:
- attn_out: bfloat16 [12288, 4608], P(('groups', 'tp', 'sp')), parts along dimension 0
There are 4 independent parts, one for each index of `groups`. A program takes and returns all parts, laid end to end along the dimension named above; an argument that names none is the same for every part. Nothing has to cross between parts.
Inputs may be any that keep to these rules, and one draw needn't show every extreme that they name: `doc_lengths`: positive lengths that sum to 3072; the largest is exactly a quarter of 3072.
All inputs are finite; a program needn't handle non-finite values.
Results may differ from a plain program's by a relative error of at most 0.024.
Values may be sent and summed in bfloat16 or wider, within the bound.
A program may use at most 128 MiB of HBM per device.

v0:
```python
import jax
import jax.numpy as jnp
from jax import lax
from jax.sharding import PartitionSpec as P

PRE_SCALE = 144
masked_low = -1e30


def partner_2(block, axis, bit):
    count = lax.axis_size(axis)
    route = []
    for low in range(count):
        high = low | 1 << bit
        if high != low and high < count:
            route += [(low, high), (high, low)]
    return lax.ppermute(block, axis, route)


def rotate(matrix, places):
    half_width = matrix.shape[1] // 2
    spread = jnp.power(
        10000.0, -(jnp.arange(half_width, dtype=jnp.float32) * (2.0 / matrix.shape[1]))
    )
    angles = places.astype(jnp.float32)[:, None] * spread[None, :]
    cosine = jnp.cos(angles)
    sine_part = jnp.sin(angles)
    lower_part = matrix[:, :half_width]
    upper_part = matrix[:, half_width:]
    return jnp.concatenate(
        [
            lower_part * cosine - upper_part * sine_part,
            upper_part * cosine + lower_part * sine_part,
        ],
        axis=1,
    )


def doc_index(places, doc_ends):
    return jnp.sum((places[:, None] >= doc_ends[None, :]).astype(jnp.int32), axis=1)


def attend(running, queries, query_places, query_docs, key_rows, value_rows, key_places, key_docs):
    query_count = queries.shape[0]
    key_count = key_rows.shape[0]
    query_block = 512
    key_block = 512
    across = key_count // key_block

    def visit_tile(step_index, carried):
        query_start = step_index // across * query_block
        key_start = step_index % across * key_block
        query_part = lax.dynamic_slice_in_dim(queries, query_start, query_block, 0)
        place_part = lax.dynamic_slice_in_dim(query_places, query_start, query_block, 0)
        docs_part = lax.dynamic_slice_in_dim(query_docs, query_start, query_block, 0)
        key_part = lax.dynamic_slice_in_dim(key_rows, key_start, key_block, 0)
        value_part = lax.dynamic_slice_in_dim(value_rows, key_start, key_block, 0)
        key_place_part = lax.dynamic_slice_in_dim(key_places, key_start, key_block, 0)
        key_docs_part = lax.dynamic_slice_in_dim(key_docs, key_start, key_block, 0)
        largest_all, denominator_all, accum_all = carried
        largest_old = lax.dynamic_slice_in_dim(largest_all, query_start, query_block, 0)
        denominator_old = lax.dynamic_slice_in_dim(denominator_all, query_start, query_block, 0)
        accum_old = lax.dynamic_slice_in_dim(accum_all, query_start, query_block, 0)
        scores = jnp.einsum("qd,kd->qk", query_part, key_part, preferred_element_type=jnp.float32)
        allowed = (key_place_part[None, :] <= place_part[:, None]) & (
            key_docs_part[None, :] == docs_part[:, None]
        )
        largest_new = jnp.maximum(
            largest_old, jnp.max(jnp.where(allowed, scores, masked_low), axis=1, keepdims=True)
        )
        weights = jnp.where(allowed, jnp.exp(scores - largest_new), 0.0)
        fading = jnp.exp(largest_old - largest_new)
        denominator_new = denominator_old * fading + jnp.sum(weights, axis=1, keepdims=True)
        accum_new = accum_old * fading + jnp.dot(
            weights.astype(jnp.bfloat16), value_part, preferred_element_type=jnp.float32
        )
        return (
            lax.dynamic_update_slice_in_dim(largest_all, largest_new, query_start, 0),
            lax.dynamic_update_slice_in_dim(denominator_all, denominator_new, query_start, 0),
            lax.dynamic_update_slice_in_dim(accum_all, accum_new, query_start, 0),
        )

    return lax.fori_loop(0, query_count // query_block * across, visit_tile, running)


def pair_up(halves, places, tp_place, half_dim):
    partner = partner_2(halves, "tp", 0)
    is_even = tp_place % 2 == 0
    lower_rows = jnp.where(is_even, halves, partner)
    upper_rows = jnp.where(is_even, partner, halves)
    key_raw = jnp.concatenate([lower_rows[:, :half_dim], upper_rows[:, :half_dim]], axis=1)
    value_rows = jnp.concatenate([lower_rows[:, half_dim:], upper_rows[:, half_dim:]], axis=1)
    key_rows = rotate(key_raw.astype(jnp.float32), places).astype(jnp.bfloat16)
    return (key_rows, value_rows)


def local(tokens, w_query, w_key, w_value, w_out, doc_lengths):
    local_rows = tokens.shape[0]
    tp_count = lax.axis_size("tp")
    sp_count = lax.axis_size("sp")
    sp_place = lax.axis_index("sp")
    tp_place = lax.axis_index("tp")
    head_dim = w_query.shape[1]
    half_dim = w_key.shape[1]
    own_rows = local_rows * tp_count
    w_input = jnp.concatenate([w_query, w_key, w_value], axis=1)
    doc_ends = jnp.cumsum(doc_lengths)
    row_ids = jnp.arange(own_rows, dtype=jnp.int32)
    query_places = (row_ids // local_rows * sp_count + sp_place) * local_rows + row_ids % local_rows
    query_docs = doc_index(query_places, doc_ends)
    produced = jnp.dot(
        lax.all_gather(tokens, "tp", axis=0, tiled=True),
        w_input,
        preferred_element_type=jnp.float32,
    )
    query_raw = produced[:, :head_dim]
    halves = produced[:, head_dim:].astype(jnp.bfloat16)
    queries = (rotate(query_raw, query_places) * PRE_SCALE ** (-0.5)).astype(jnp.bfloat16)
    key_rows, value_rows = pair_up(halves, query_places, tp_place, half_dim)
    initial = (
        jnp.full((own_rows, 1), masked_low, jnp.float32),
        jnp.zeros((own_rows, 1), jnp.float32),
        jnp.zeros((own_rows, head_dim), jnp.float32),
    )
    shard_part = (
        lax.all_gather(key_rows, "sp", axis=0, tiled=True),
        lax.all_gather(value_rows, "sp", axis=0, tiled=True),
    )
    gathered_ids = jnp.arange(shard_part[0].shape[0], dtype=jnp.int32)
    source = gathered_ids // own_rows
    within = gathered_ids % own_rows
    places = (within // local_rows * sp_count + source) * local_rows + within % local_rows
    finished = attend(
        initial,
        queries,
        query_places,
        query_docs,
        shard_part[0],
        shard_part[1],
        places,
        doc_index(places, doc_ends),
    )
    largest_all, denominator_all, accum_all = finished
    attended = (accum_all / denominator_all).astype(jnp.bfloat16)
    return lax.psum_scatter(
        jnp.dot(attended, w_out, preferred_element_type=jnp.float32).astype(jnp.bfloat16),
        "tp",
        scatter_dimension=0,
        tiled=True,
    )


def solution(mesh):
    placed = (
        P(("groups", "tp", "sp"), None),
        P(None, "tp"),
        P(None, "tp"),
        P(None, "tp"),
        P("tp", None),
        P("groups"),
    )
    return jax.shard_map(
        local,
        mesh=mesh,
        in_specs=placed,
        out_specs=P(("groups", "tp", "sp"), None),
        check_vma=False,
    )
```

profile of v0, /device:TPU:37, one launch (start us, length us, event | category | flops | bytes accessed | tf_op | source)
XLA Modules:
  0.0 510.9 jit_solution(526202389130017574)
XLA Ops:
  7.4 2.3 copy.12
  9.7 1.4 copy.13
  11.1 185.4 %all-gather.2.cloned.1.call-done = bf16[1536,4608]{1,0:T(8,128)(2,1)} async-done(((bf16[48,4608]{1,0:T(8,128)(2,1)}), bf16[1536,4608]{1,0:T(8,128)(2,1)}) %all-gather.2.cloned.1.call-update) | async-done | bytes 14155792 | tf_op jit(solution)/shard_map/all_gather | solution.py:112
  196.5 9.7 %convolution_bitcast_fusion = f32[1536,256]{0,1:T(8,128)S(1)} fusion(bf16[1536,4608]{1,0:T(8,128)(2,1)} %all-gather.2.cloned.1.call-done, bf16[4608,64]{1,0:T(8,128)(2,1)} %copy.13, bf16[4608,64]{1,0:T(8,128)(2,1)} %copy.12, bf16[4608,128]{1,0:T(8,128)(2,1)} %param.9), kind=kOutput, calls=%fused_computation.29 | convolution fusion | flops 3630956544 | bytes 18087936 | tf_op jit(solution)/shard_map/dot_general | solution.py:111
  207.0 1.3 reduce-window.8
  208.4 1.3 convert_reduce_fusion.1
  209.7 1.4 convert_reduce_fusion
  211.1 4.7 collective-permute-done
  216.0 4.2 all_gather.11
  220.3 1.7 fusion.37
  222.0 2.4 all_gather.10
  224.5 0.8 fusion.25
  225.9 96.6 %while.19 = (s32[]{:T(128)}, f32[1536,1]{0,1:T(1,128)S(1)}, f32[1536,1]{0,1:T(1,128)}, f32[1536,128]{1,0:T(8,128)S(1)}, s32[3072]{0:T(1024)}, /*index=5*/s32[153...) while((s32[]{:T(128)}, f32[1536,1]{0,1:T(1,128)S(1)}, ...), condition=%wide.region_6.7_spmd, body=%wide.region_3.6_spmd.sunk | while | flops 138806304 | bytes 4209108 | solution.py:83
  227.4 0.8 dynamic_slice.139
  228.9 1.3 select_reduce_fusion.2
  232.8 0.8 dynamic_slice.139
  234.3 1.3 select_reduce_fusion.2
  238.1 0.8 dynamic_slice.139
  239.7 1.3 select_reduce_fusion.2
  243.5 0.8 dynamic_slice.139
  245.0 1.3 select_reduce_fusion.2
  247.4 0.8 dynamic_slice.141
  248.1 0.8 dynamic_slice.142
  248.9 0.8 dynamic_slice.139
  250.4 1.3 select_reduce_fusion.2
  252.8 0.8 dynamic_slice.141
  253.5 0.8 dynamic_slice.142
  254.3 0.8 dynamic_slice.139
  255.8 1.3 select_reduce_fusion.2
  259.6 0.8 dynamic_slice.139
  261.2 1.3 select_reduce_fusion.2
  265.0 0.8 dynamic_slice.139
  266.5 1.3 select_reduce_fusion.2
  270.4 0.8 dynamic_slice.139
  271.9 1.3 select_reduce_fusion.2
  275.8 0.8 dynamic_slice.139
  277.3 1.3 select_reduce_fusion.2
  279.6 0.8 dynamic_slice.141
  280.4 0.8 dynamic_slice.142
  281.1 0.8 dynamic_slice.139
  282.7 1.3 select_reduce_fusion.2
  285.0 0.8 dynamic_slice.141
  285.8 0.8 dynamic_slice.142
  286.5 0.8 dynamic_slice.139
  288.0 1.3 select_reduce_fusion.2
  291.9 0.8 dynamic_slice.139
  293.4 1.3 select_reduce_fusion.2
  297.2 0.8 dynamic_slice.139
  298.8 1.3 select_reduce_fusion.2
  301.1 0.8 dynamic_slice.141
  302.6 0.8 dynamic_slice.139
  304.1 1.3 select_reduce_fusion.2
  308.0 0.8 dynamic_slice.139
  309.5 1.3 select_reduce_fusion.2
  311.8 0.8 dynamic_slice.141
  312.6 0.8 dynamic_slice.142
  313.4 0.8 dynamic_slice.139
  314.9 1.3 select_reduce_fusion.2
  317.2 0.8 dynamic_slice.141
  318.0 0.8 dynamic_slice.142
  318.7 0.8 dynamic_slice.139
  320.3 1.3 select_reduce_fusion.2
  323.3 7.4 %convolution_convert_fusion = bf16[1536,4608]{1,0:T(8,128)(2,1)} fusion(bf16[128,4608]{1,0:T(8,128)(2,1)S(1)} %copy-done, f32[1536,128]{1,0:T(8,128)S(1)} %get-tuple-element.273, f32[1536]{0:T(1024)S(1)} %reduce), kind=kOutput, calls=%fused_computation.28 | convolution fusion | flops 1819410432 | bytes 16128000 | tf_op jit(solution)/shard_map/dot_general | solution.py:146
  330.8 173.2 %reduce-scatter.2.cloned.1.call-done = bf16[48,4608]{1,0:T(8,128)(2,1)} async-done(((bf16[1536,4608]{1,0:T(8,128)(2,1)}), bf16[48,4608]{1,0:T(8,128)(2,1)}) %reduce-scatter.2.cloned.1.call-update) | async-done | bytes 442384 | tf_op jit(solution)/shard_map/reduce_scatter | solution.py:145
  (250 shorter events, 51.2 us)
Async XLA Ops:
  6.5 316.8 %copy-start = (bf16[128,4608]{1,0:T(8,128)(2,1)S(1)}, bf16[128,4608]{1,0:T(8,128)(2,1)}, u32[]{:S(2)}) copy-start(bf16[128,4608]{1,0:T(8,128)(2,1)} %param.12) | copy-start | bytes 3538948
  6.6 3.1 copy-start.1
  6.6 190.0 %all-gather.2.cloned.1.call-start = ((), (), s32[]{:S(2)}) async-start(), calls=%async_computation.1 | async-start | bytes 14598144 | tf_op jit(solution)/shard_map/all_gather | solution.py:112
  7.3 496.7 %reduce-scatter.2.cloned.1.call-start = ((), (), s32[]{:S(2)}) async-start(), calls=%async_computation.2 | async-start | bytes 14598144 | tf_op jit(solution)/shard_map/reduce_scatter | solution.py:145
  11.1 197.2 %copy-start.3 = (s32[1536]{0:T(1024)}, s32[1536]{0:T(1024)S(1)}, u32[]{:S(2)}) copy-start(s32[1536]{0:T(1024)S(1)} %fusion.69) | copy-start | bytes 18436
  206.3 9.5 %collective-permute-start = (bf16[1536,128]{0,1:T(8,128)(2,1)S(1)}, bf16[1536,128]{0,1:T(8,128)(2,1)S(1)}, u32[]{:S(2)}, u32[]{:S(2)}) collective-permute-start(bf16[1536,128]{0,1:T(8,128)(2,1)S(1)} %slice.58), channel_id=1, source_target_pairs={{0,2},{2,0},{4,6},{6,4},{8,10},{10,8},{12,14},{14,12},{16,18},{18,... | collective-permute-start | bytes 1179656 | tf_op jit(solution)/shard_map/ppermute | solution.py:17
  208.4 2.7 copy-start.2
  215.9 4.4 copy-start.6
  227.4 3.2 copy-start.4
  230.6 0.6 copy-start.5
  232.8 3.2 copy-start.4
  236.0 0.6 copy-start.5
  238.1 3.2 copy-start.4
  241.4 0.6 copy-start.5
  243.5 3.2 copy-start.4
  246.7 0.6 copy-start.5
  248.9 3.2 copy-start.4
  252.1 0.6 copy-start.5
  254.3 3.2 copy-start.4
  257.5 0.6 copy-start.5
  259.6 3.2 copy-start.4
  262.9 0.6 copy-start.5
  265.0 3.2 copy-start.4
  268.2 0.6 copy-start.5
  270.4 3.2 copy-start.4
  273.6 0.6 copy-start.5
  275.7 3.2 copy-start.4
  279.0 0.6 copy-start.5
  281.1 3.2 copy-start.4
  284.3 0.6 copy-start.5
  286.5 3.2 copy-start.4
  289.7 0.6 copy-start.5
  291.9 3.2 copy-start.4
  295.1 0.6 copy-start.5
  297.2 3.2 copy-start.4
  300.5 0.6 copy-start.5
  302.6 3.2 copy-start.4
  305.8 0.6 copy-start.5
  308.0 3.2 copy-start.4
  311.2 0.6 copy-start.5
  313.4 3.2 copy-start.4
  316.6 0.6 copy-start.5
  318.7 3.2 copy-start.4
  322.0 0.6 copy-start.5
Sparse Core Ops, SparseCore 0:
  9.2 187.3 all-gather.1
  330.9 173.0 reduce-scatter.1
where the time goes:
time: 514 us; the launch traced here: 511 us
  waiting for transfers between devices  364 us (71%)
  local copies, waits for them, and re-layouts  59 us (11%)
  matrix products  51 us (10%)
  other arithmetic  14.6 us (3%)
  between operations  13.6 us (3%)
  blocking collectives  6.61 us (1%)
    all_gather x1, waiting for transfers between devices, local(): lax.all_gather(tokens, 'tp', axis=0, tiled=True)  185 us
    reduce_scatter x1, waiting for transfers between devices, local(): lax.psum_scatter(jnp.dot(attended, w_out, preferred_element_type=jnp.floa...  173 us
    dot_general x18, matrix products, visit_tile(): jnp.einsum('qd,kd->qk', query_part, key_part, preferred_element_type=jnp....  23.4 us
    dynamic_slice x18, local copies, waits for them, and re-layouts, visit_tile(): lax.dynamic_slice_in_dim(query_docs, query_start, query_block, 0)  13.8 us
    dynamic_slice x18, local copies, waits for them, and re-layouts, visit_tile(): key_docs_part = lax.dynamic_slice_in_dim(key_docs, key_start, key_block, 0)  13.6 us
    dynamic_slice x18, local copies, waits for them, and re-layouts, visit_tile(): lax.dynamic_slice_in_dim(query_places, query_start, query_block, 0)  13.5 us
    dynamic_slice x18, local copies, waits for them, and re-layouts, visit_tile(): lax.dynamic_slice_in_dim(key_places, key_start, key_block, 0)  13.5 us
    dot_general x18, matrix products, visit_tile(): jnp.dot(weights.astype(jnp.bfloat16), value_part, preferred_element_type=...  10.5 us
  transfers between devices with their start and end apart: 3, of which 3 were waited for; matrix products, arithmetic and copies ran while one was open for 2% of the time, Pallas kernels for 0%

commit v1 on v0

--- a/solution.py
+++ b/solution.py
@@ -1,3 +1,4 @@
+import functools
 import jax
 import jax.numpy as jnp
 from jax import lax
@@ -5,6 +6,19 @@
 
 PRE_SCALE = 144
 masked_low = -1e30
+
+
+def proceed_slots(field, net_axis):
+    return jax.lax.all_to_all(
+        jnp.concatenate(jax.lax.axis_size(net_axis) * [field], axis=0),
+        net_axis,
+        split_axis=0,
+        concat_axis=0,
+        tiled=True,
+    )
+
+
+recover_the_points = functools.partial(proceed_slots, net_axis="tp")
 
 
 def partner_2(block, axis, bit):
@@ -108,11 +122,7 @@
     row_ids = jnp.arange(own_rows, dtype=jnp.int32)
     query_places = (row_ids // local_rows * sp_count + sp_place) * local_rows + row_ids % local_rows
     query_docs = doc_index(query_places, doc_ends)
-    produced = jnp.dot(
-        lax.all_gather(tokens, "tp", axis=0, tiled=True),
-        w_input,
-        preferred_element_type=jnp.float32,
-    )
+    produced = jnp.dot(recover_the_points(tokens), w_input, preferred_element_type=jnp.float32)
     query_raw = produced[:, :head_dim]
     halves = produced[:, head_dim:].astype(jnp.bfloat16)
     queries = (rotate(query_raw, query_places) * PRE_SCALE ** (-0.5)).astype(jnp.bfloat16)

time: 514 us -> 1620 us (3.15)
  waiting for transfers between devices: 364 us -> 1370 us
  starting transfers between devices: 0.21 us -> 51.4 us
  other arithmetic: 14.6 us -> 37.8 us
  local copies, waits for them, and re-layouts: 59 us -> 80.2 us
    all_to_all x0 -> x1, waiting for transfers between devices: none -> 1190 us  [proceed_slots(): jax.lax.all_to_all(jnp.concatenate(jax.lax.axis_size(net_axis) * [field],...]
    all_gather x1 -> x0, waiting for transfers between devices: 185 us -> none  [local(): lax.all_gather(tokens, 'tp', axis=0, tiled=True)]
    all_to_all x0 -> x1, starting transfers between devices: none -> 33.3 us  [proceed_slots(): jax.lax.all_to_all(jnp.concatenate(jax.lax.axis_size(net_axis) * [field],...]
    dynamic_update_slice x18, other arithmetic: 0.45 us -> 22.9 us  [visit_tile(): lax.dynamic_update_slice_in_dim(denominator_all, denominator_new, query_s...]
    unnamed x12 -> x47, local copies, waits for them, and re-layouts: 3.72 us -> 25.2 us
    ppermute x1, starting transfers between devices: 0.14 us -> 18 us  [partner_2(): return lax.ppermute(block, axis, route)]
  transfers between devices with their start and end apart: 3 -> 3, of which waited for: 3 -> 3; matrix products, arithmetic and copies ran while one was open for 2% -> 0% of each run, Pallas kernels for 0% -> 0%
where the time goes in v1:
time: 1620 us
  waiting for transfers between devices  1370 us (85%)
  local copies, waits for them, and re-layouts  80.2 us (5%)
  starting transfers between devices  51.4 us (3%)
  matrix products  50.5 us (3%)
  other arithmetic  37.8 us (2%)
    all_to_all x1, waiting for transfers between devices, proceed_slots(): jax.lax.all_to_all(jnp.concatenate(jax.lax.axis_size(net_axis) * [field],...  1190 us
    reduce_scatter x1, waiting for transfers between devices, local(): lax.psum_scatter(jnp.dot(attended, w_out, preferred_element_type=jnp.floa...  178 us
    all_to_all x1, starting transfers between devices, proceed_slots(): jax.lax.all_to_all(jnp.concatenate(jax.lax.axis_size(net_axis) * [field],...  33.3 us
  transfers between devices with their start and end apart: 3, of which 3 were waited for; matrix products, arithmetic and copies ran while one was open for 0% of the time, Pallas kernels for 0%

profile of v1, /device:TPU:37, one launch (start us, length us, event | category | flops | bytes accessed | tf_op | source)
XLA Modules:
  0.0 1617.1 jit_solution(7821138589711460142)
XLA Ops:
  6.6 1.2 constant_dynamic-update-slice_fusion.33
  7.7 1.0 constant_dynamic-update-slice_fusion.32
  8.8 1.0 constant_dynamic-update-slice_fusion.31
  9.8 1.0 constant_dynamic-update-slice_fusion.30
  10.9 1.0 constant_dynamic-update-slice_fusion.29
  13.0 1.0 constant_dynamic-update-slice_fusion.27
  14.0 1.0 constant_dynamic-update-slice_fusion.26
  15.1 1.0 constant_dynamic-update-slice_fusion.25
  17.1 1.0 constant_dynamic-update-slice_fusion.23
  18.2 1.0 constant_dynamic-update-slice_fusion.22
  19.2 1.0 constant_dynamic-update-slice_fusion.21
  21.3 1.0 constant_dynamic-update-slice_fusion.19
  24.1 5.1 copy-done.2
  29.2 33.3 %all-to-all-start = ((bf16[32,48,4608]{2,1,0:T(8,128)(2,1)}), bf16[32,48,4608]{2,1,0:T(8,128)(2,1)}, u32[]{:S(2)}, u32[]{:S(2)}) async-start(bf16[32,48,4608]{2,1,0:T(8,128)(2,1)} %bitcast.18), calls=%async_computation | async-start | bytes 28311552 | tf_op jit(solution)/shard_map/all_to_all | solution.py:12
  62.6 1.4 copy.12
  64.1 1.4 copy.13
  65.5 1190.9 %all-to-all-done = bf16[32,48,4608]{2,1,0:T(8,128)(2,1)} async-done(((bf16[32,48,4608]{2,1,0:T(8,128)(2,1)}), bf16[32,48,4608]{2,1,0:T(8,128)(2,1)}, u32[]{:S(2)}, u32[]{:S(2)}) %all-to-all-start) | async-done | bytes 14155808 | tf_op jit(solution)/shard_map/all_to_all | solution.py:12
  1256.4 9.7 fusion.20
  1266.2 18.0 %collective-permute-start = (bf16[1536,128]{0,1:T(8,128)(2,1)S(1)}, bf16[1536,128]{0,1:T(8,128)(2,1)S(1)}, u32[]{:S(2)}, u32[]{:S(2)}) collective-permute-start(bf16[1536,128]{0,1:T(8,128)(2,1)S(1)} %slice.58), channel_id=1, source_target_pairs={{0,2},{2,0},{4,6},{6,4},{8,10},{10,8},{12,14},{14,12},{16,18},{18,... | collective-permute-start | bytes 1179656 | tf_op jit(solution)/shard_map/ppermute | solution.py:31
  1284.8 1.3 reduce-window.8
  1286.2 1.3 convert_reduce_fusion.1
  1287.5 1.4 convert_reduce_fusion
  1290.1 9.6 all_gather.7
  1299.8 2.4 fusion.38
  1302.2 2.4 all_gather.6
  1306.1 117.7 %while.19 = (s32[]{:T(128)}, f32[1536,1]{0,1:T(1,128)S(1)}, f32[1536,1]{0,1:T(1,128)}, f32[1536,128]{1,0:T(8,128)S(1)}, s32[3072]{0:T(1024)}, /*index=5*/s32[153...) while((s32[]{:T(128)}, f32[1536,1]{0,1:T(1,128)S(1)}, ...), condition=%wide.region_6.7_spmd, body=%wide.region_3.6_spmd.sunk | while | flops 138806304 | bytes 4159900 | solution.py:97
  1309.1 1.3 select_reduce_fusion.2
  1310.8 1.3 constant_dynamic-update-slice_fusion.37
  1315.6 1.3 select_reduce_fusion.2
  1317.3 1.3 constant_dynamic-update-slice_fusion.37
  1322.2 1.3 select_reduce_fusion.2
  1323.8 1.3 constant_dynamic-update-slice_fusion.37
  1328.7 1.3 select_reduce_fusion.2
  1330.3 1.3 constant_dynamic-update-slice_fusion.37
  1335.2 1.3 select_reduce_fusion.2
  1336.9 1.3 constant_dynamic-update-slice_fusion.37
  1341.7 1.3 select_reduce_fusion.2
  1343.4 1.3 constant_dynamic-update-slice_fusion.37
  1348.3 1.3 select_reduce_fusion.2
  1349.9 1.3 constant_dynamic-update-slice_fusion.37
  1354.8 1.3 select_reduce_fusion.2
  1356.5 1.3 constant_dynamic-update-slice_fusion.37
  1361.4 1.3 select_reduce_fusion.2
  1363.0 1.3 constant_dynamic-update-slice_fusion.37
  1367.9 1.3 select_reduce_fusion.2
  1369.6 1.3 constant_dynamic-update-slice_fusion.37
  1374.5 1.3 select_reduce_fusion.2
  1376.1 1.3 constant_dynamic-update-slice_fusion.37
  1381.0 1.3 select_reduce_fusion.2
  1382.7 1.3 constant_dynamic-update-slice_fusion.37
  1387.6 1.3 select_reduce_fusion.2
  1389.2 1.3 constant_dynamic-update-slice_fusion.37
  1394.1 1.3 select_reduce_fusion.2
  1395.8 1.3 constant_dynamic-update-slice_fusion.37
  1400.7 1.3 select_reduce_fusion.2
  1402.3 1.3 constant_dynamic-update-slice_fusion.37
  1407.2 1.3 select_reduce_fusion.2
  1408.8 1.3 constant_dynamic-update-slice_fusion.37
  1413.7 1.3 select_reduce_fusion.2
  1415.4 1.3 constant_dynamic-update-slice_fusion.37
  1420.3 1.3 select_reduce_fusion.2
  1421.9 1.3 constant_dynamic-update-slice_fusion.37
  1424.5 7.4 convolution_convert_fusion
  1431.9 178.3 %reduce-scatter.2.cloned.1.call-done = bf16[48,4608]{1,0:T(8,128)(2,1)} async-done(((bf16[1536,4608]{1,0:T(8,128)(2,1)}), bf16[48,4608]{1,0:T(8,128)(2,1)}) %reduce-scatter.2.cloned.1.call-update) | async-done | bytes 442384 | tf_op jit(solution)/shard_map/reduce_scatter | solution.py:155
  (213 shorter events, 79.1 us)
Async XLA Ops:
  6.5 1417.9 %copy-start = (bf16[128,4608]{1,0:T(8,128)(2,1)S(1)}, bf16[128,4608]{1,0:T(8,128)(2,1)}, u32[]{:S(2)}) copy-start(bf16[128,4608]{1,0:T(8,128)(2,1)} %param.12) | copy-start | bytes 3538948
  6.6 16.9 %copy-start.1 = (bf16[48,4608]{1,0:T(8,128)(2,1)S(1)}, bf16[48,4608]{1,0:T(8,128)(2,1)}, u32[]{:S(2)}) copy-start(bf16[48,4608]{1,0:T(8,128)(2,1)} %param.8) | copy-start | bytes 1327108
  24.1 5.1 copy-start.2
  29.2 33.4 %copy-start.3 = (bf16[4608,64]{0,1:T(8,128)(2,1)S(1)}, bf16[4608,64]{0,1:T(8,128)(2,1)}, u32[]{:S(2)}) copy-start(bf16[4608,64]{0,1:T(8,128)(2,1)} %param.10) | copy-start | bytes 1769476
  29.2 34.8 %copy-start.4 = (bf16[4608,64]{0,1:T(8,128)(2,1)S(1)}, bf16[4608,64]{0,1:T(8,128)(2,1)}, u32[]{:S(2)}) copy-start(bf16[4608,64]{0,1:T(8,128)(2,1)} %param.11) | copy-start | bytes 1769476
  29.2 1227.2 %all-to-all-start = ((bf16[32,48,4608]{2,1,0:T(8,128)(2,1)}), bf16[32,48,4608]{2,1,0:T(8,128)(2,1)}, u32[]{:S(2)}, u32[]{:S(2)}) async-start(bf16[32,48,4608]{2,1,0:T(8,128)(2,1)} %bitcast.18), calls=%async_computation | async-start | bytes 28311552 | tf_op jit(solution)/shard_map/all_to_all | solution.py:12
  62.6 1547.7 %reduce-scatter.2.cloned.1.call-start = ((), (), s32[]{:S(2)}) async-start(), calls=%async_computation.2 | async-start | bytes 14598144 | tf_op jit(solution)/shard_map/reduce_scatter | solution.py:155
  65.5 1220.7 %copy-start.6 = (s32[1536]{0:T(1024)}, s32[1536]{0:T(1024)S(1)}, u32[]{:S(2)}) copy-start(s32[1536]{0:T(1024)S(1)} %fusion.70) | copy-start | bytes 18436
  1266.2 23.7 %collective-permute-start = (bf16[1536,128]{0,1:T(8,128)(2,1)S(1)}, bf16[1536,128]{0,1:T(8,128)(2,1)S(1)}, u32[]{:S(2)}, u32[]{:S(2)}) collective-permute-start(bf16[1536,128]{0,1:T(8,128)(2,1)S(1)} %slice.58), channel_id=1, source_target_pairs={{0,2},{2,0},{4,6},{6,4},{8,10},{10,8},{12,14},{14,12},{16,18},{18,... | collective-permute-start | bytes 1179656 | tf_op jit(solution)/shard_map/ppermute | solution.py:31
  1286.2 2.7 copy-start.5
Sparse Core Ops, SparseCore 0:
  1432.1 178.1 reduce-scatter.1
